TPU v7x, 256 devices: a whole 4x4x8 slice. The times are simulated.
256 devices in a mesh: expert: 64 (over x, z, core), mp: 4 (over y).
Axes of the slice: x: 4, y: 4, z: 8, core: 2. Of those that a mesh axis runs over, the one named last changes fastest.
Arguments:
- tokens: bfloat16 [1536, 6144], P('expert', 'mp'), may hold values from -6 to 6
- mix_weights: float32 [1536, 2], P('expert'), may hold values from 0.2 to 1
- routes: int32 [1536, 2], P('expert'), may hold values from 0 to 7, as said below
- w_gate: bfloat16 [64, 6144, 1024], P('expert', None, 'mp'), may hold values from -0.078125 to 0.078125
- w_up: bfloat16 [64, 6144, 1024], P('expert', None, 'mp'), may hold values from -0.078125 to 0.078125
- w_down: bfloat16 [64, 1024, 6144], P('expert', 'mp'), may hold values from -0.0625 to 0.0625
Outputs:
- mixed_out: bfloat16 [1536, 6144], P('expert', 'mp')
Inputs may be any that keep to these rules, and one draw needn't show every extreme that they name: `routes`: each row names 2 different experts, and every expert is named by some row. Among the 24 rows of one index of the expert axis no expert is named more than 12 times, and on some indices one is named exactly 12 times.
All inputs are finite; a program needn't handle non-finite values.
Results may differ from a plain program's by a relative error of at most 0.011.
Values may be sent and summed in bfloat16 or wider, within the bound.
No kernel may reach another device: no remote copies, remote signals or barrier semaphores. Data moves between devices by JAX's collectives and lax.ppermute only.
A program may use at most 128 MiB of HBM per device.

v0:
```python
import jax
import jax.numpy as jnp
from jax import lax
from jax.sharding import Mesh
from jax.sharding import PartitionSpec as P

EXPERTS = 8
TOP = 2
EXPERT = ("expert_0", "expert_1", "expert_2")


def joined_along(pieces, dim):
    shape = list(pieces.shape[1:])
    shape[dim] *= pieces.shape[0]
    return jnp.moveaxis(pieces, 0, dim).reshape(shape)


def copy_for_each(value, axis):
    size = lax.axis_size(axis)
    return lax.all_to_all(
        jnp.broadcast_to(value[None], (size, *value.shape)), axis, 0, 0, tiled=True
    )


def collect(value, axis, dim):
    return joined_along(copy_for_each(value, axis), dim)


def split_up(value, dim, size):
    shape = value.shape
    pieces = value.reshape(*shape[:dim], size, shape[dim] // size, *shape[dim + 1 :])
    return jnp.moveaxis(pieces, dim, 0)


def exchange_in_order(pieces, axes, sequence):
    shape = [lax.axis_size(a) for a in axes]
    pieces = pieces.reshape(*shape, *pieces.shape[1:])
    for k in sequence:
        pieces = lax.all_to_all(pieces, axes[k], split_axis=k, concat_axis=k, tiled=True)
    return pieces.reshape(-1, *pieces.shape[len(axes) :])


def exchange_by_chip(value, groups, sequence, split_dim, concat_dim):
    size = lax.axis_size(groups[0]) * lax.axis_size(groups[1])
    pieces = split_up(value, split_dim, size)
    return joined_along(exchange_in_order(pieces, groups, sequence), concat_dim)


def pack_rows(pick_tokens, features, repeats):
    packed = jnp.einsum(
        "tem,tc->emc", pick_tokens, features, preferred_element_type=jnp.float32
    ).astype(jnp.bfloat16)
    spread = jnp.broadcast_to(packed[:, None], (packed.shape[0], repeats) + packed.shape[1:])
    return spread.reshape((packed.shape[0] * repeats,) + packed.shape[1:])


def activate(gate_act, up_act):
    return (jax.nn.silu(gate_act) * up_act).astype(jnp.bfloat16)


def local(tokens, mix_weights, routes, w_gate, w_up, w_down):
    tok_rows = tokens.shape[0]
    senders = lax.axis_size(EXPERT)
    group_size = senders // EXPERTS
    capacity = 5 * tok_rows * senders * TOP // (4 * EXPERTS)
    most_rows = tok_rows // 2
    labels = jnp.arange(EXPERTS, dtype=jnp.int32)
    flat_ids = routes.reshape(-1)
    marked = (flat_ids[:, None] == labels[None, :]).astype(jnp.int32)
    earlier = jnp.cumsum(marked, axis=0) - marked
    local_rank = jnp.sum(earlier * marked, axis=1)
    counts = jnp.sum(marked, axis=0)
    count_grid = collect(counts[None, :], EXPERT, 0)
    my_index = lax.axis_index(EXPERT)
    sender_ids = jnp.arange(senders, dtype=jnp.int32)
    lower_mask = (sender_ids[:, None] < my_index).astype(jnp.int32)
    offsets = jnp.sum(count_grid * lower_mask, axis=0)
    slot_ids = jnp.sum(marked * offsets[None, :], axis=1) + local_rank
    keep_mask = (slot_ids < capacity).astype(jnp.int32)
    rank_hit = (local_rank[:, None] == jnp.arange(most_rows, dtype=jnp.int32)[None, :]).astype(
        jnp.int32
    ) * keep_mask[:, None]
    assign_pick = marked[:, :, None] * rank_hit[:, None, :]
    pick_tokens = jnp.sum(assign_pick.reshape(tok_rows, TOP, EXPERTS, most_rows), axis=1).astype(
        jnp.bfloat16
    )
    weighted = assign_pick.astype(jnp.float32) * mix_weights.reshape(-1)[:, None, None]
    combine_w = jnp.sum(weighted.reshape(tok_rows, TOP, EXPERTS * most_rows), axis=1)
    gate_rows = w_gate[0]
    up_rows = w_up[0]
    down_rows = w_down[0]
    arrived = lax.all_to_all(
        pack_rows(pick_tokens, tokens, group_size), EXPERT, split_axis=0, concat_axis=0, tiled=True
    )
    arrived_rows = arrived.reshape(senders * most_rows, arrived.shape[2])
    my_expert = my_index // group_size
    column_counts = jnp.sum(count_grid * (labels[None, :] == my_expert).astype(jnp.int32), axis=1)
    starts = jnp.cumsum(column_counts) - column_counts
    slot_pos = jnp.arange(capacity, dtype=jnp.int32)
    slot_ends = starts + column_counts
    source_of = jnp.minimum(
        jnp.sum((slot_ends[None, :] <= slot_pos[:, None]).astype(jnp.int32), axis=1), senders - 1
    )
    source_hit = (sender_ids[None, :] == source_of[:, None]).astype(jnp.int32)
    start_of = jnp.sum(source_hit * starts[None, :], axis=1)
    slot_valid = slot_pos < jnp.sum(column_counts)
    fetch_idx = jnp.where(slot_valid, source_of * most_rows + slot_pos - start_of, 0)
    in_rows = jnp.where(
        slot_valid[:, None], jnp.take(arrived_rows, fetch_idx, axis=0), jnp.zeros((), jnp.bfloat16)
    )
    shard_piece = lax.all_gather(in_rows, "mp", axis=1, tiled=True)
    gate_act = jnp.dot(shard_piece, gate_rows, preferred_element_type=jnp.float32)
    up_act = jnp.dot(shard_piece, up_rows, preferred_element_type=jnp.float32)
    hidden = activate(gate_act, up_act)
    part_sum = jnp.dot(hidden, down_rows, preferred_element_type=jnp.float32)
    reduced = lax.psum_scatter(part_sum.astype(jnp.bfloat16), "mp", scatter_dimension=1, tiled=True)
    out_width = reduced.shape[1]
    buffer_pos = jnp.arange(most_rows, dtype=jnp.int32)
    slot_back = starts[:, None] + buffer_pos[None, :]
    back_valid = (buffer_pos[None, :] < column_counts[:, None]) & (slot_back < capacity)
    back_idx = jnp.where(back_valid, slot_back, 0).reshape(-1)
    back_rows = jnp.where(
        back_valid.reshape(-1)[:, None],
        jnp.take(reduced, back_idx, axis=0),
        jnp.zeros((), jnp.bfloat16),
    )
    returned = exchange_by_chip(
        back_rows.reshape(senders, most_rows, out_width),
        (("expert_0", "expert_1"), "expert_2"),
        (1, 0),
        0,
        0,
    )
    summed = jnp.sum(
        returned.reshape(EXPERTS, group_size, most_rows, out_width).astype(jnp.float32), axis=1
    )
    result = jnp.dot(
        combine_w, summed.reshape(EXPERTS * most_rows, out_width), precision=lax.Precision.HIGHEST
    )
    return result.astype(jnp.bfloat16)


def solution(mesh):
    torus = Mesh(
        mesh.devices.reshape(4, 8, 2, mesh.shape["mp"]), ("expert_0", "expert_1", "expert_2", "mp")
    )
    placed = (
        P(EXPERT, "mp"),
        P(EXPERT, None),
        P(EXPERT, None),
        P(EXPERT, None, "mp"),
        P(EXPERT, None, "mp"),
        P(EXPERT, "mp", None),
    )
    return jax.shard_map(
        local, mesh=torus, in_specs=placed, out_specs=P(EXPERT, "mp"), check_vma=False
    )
```

profile of v0, /device:TPU:6, one launch (start us, length us, event | category | flops | bytes accessed | tf_op | source)
XLA Modules:
  0.0 377.2 jit_solution(595688700204690243)
XLA Ops:
  8.3 12.2 %all-to-all-start = ((s32[64,1,8]{2,1,0:T(1,128)}), s32[64,1,8]{2,1,0:T(1,128)S(1)}, u32[]{:S(2)}, u32[]{:S(2)}) async-start(s32[64,1,8]{2,1,0:T(1,128)} %broadcast_in_dim.86), calls=%async_computation | async-start | bytes 65536 | tf_op jit(solution)/shard_map/all_to_all | solution.py:20
  21.3 6.7 %all-to-all-done = s32[64,1,8]{2,1,0:T(1,128)S(1)} async-done(((s32[64,1,8]{2,1,0:T(1,128)}), s32[64,1,8]{2,1,0:T(1,128)S(1)}, u32[]{:S(2)}, u32[]{:S(2)}) %all-to-all-start) | async-done | bytes 2080 | tf_op jit(solution)/shard_map/all_to_all | solution.py:20
  30.5 2.1 broadcast_in_dim.93
  32.6 7.5 %all-to-all-start.1 = ((bf16[64,12,1536]{2,1,0:T(8,128)(2,1)}), bf16[64,12,1536]{2,1,0:T(8,128)(2,1)}, u32[]{:S(2)}, u32[]{:S(2)}) async-start(bf16[64,12,1536]{2,1,0:T(8,128)(2,1)} %bitcast.37), calls=%async_computation.1 | async-start | bytes 6291456 | tf_op jit(solution)/shard_map/all_to_all | solution.py:92
  41.9 68.9 %all-to-all-done.1 = bf16[64,12,1536]{2,1,0:T(8,128)(2,1)} async-done(((bf16[64,12,1536]{2,1,0:T(8,128)(2,1)}), bf16[64,12,1536]{2,1,0:T(8,128)(2,1)}, u32[]{:S(2)}, u32[]{:S(2)}) %all-to-all-start.1) | async-done | bytes 2359328 | tf_op jit(solution)/shard_map/all_to_all | solution.py:92
  110.9 4.9 %reshape.343 = bf16[768,1536]{1,0:T(8,128)(2,1)} reshape(bf16[64,12,1536]{2,1,0:T(8,128)(2,1)} %all-to-all-done.1) | data formatting | bytes 4718592 | tf_op jit(solution)/shard_map/reshape | solution.py:95
  115.8 6.4 %gather_fusion = bf16[480,1536]{1,0:T(8,128)(2,1)} fusion(bf16[768,1536]{1,0:T(8,128)(2,1)} %reshape.343, s32[1024]{0:T(1024)S(1)} %pad_clamp_fusion.1), kind=kCustom, calls=%fused_computation | custom fusion | bytes 2951040 | tf_op jit(solution)/shard_map/jit(_take)/gather | solution.py:109
  122.1 2.8 select_select_fusion.1
  125.1 63.9 %all-gather.2.cloned.1.call-done = bf16[480,6144]{1,0:T(8,128)(2,1)} async-done(((bf16[480,1536]{1,0:T(8,128)(2,1)}), bf16[480,6144]{1,0:T(8,128)(2,1)}) %all-gather.2.cloned.1.call-update) | async-done | bytes 5898256 | tf_op jit(solution)/shard_map/all_gather | solution.py:111
  189.1 5.4 %fusion.3 = f32[480,256]{1,0:T(8,128)S(1)} fusion(bf16[480,6144]{1,0:T(8,128)(2,1)} %all-gather.2.cloned.1.call-done, bf16[1,6144,256]{2,1,0:T(8,128)(2,1)} %param.9), kind=kOutput, calls=%fused_computation.8 | convolution fusion | flops 1509949440 | bytes 9535488 | tf_op jit(solution)/shard_map/dot_general | solution.py:112
  195.3 1.7 fusion.8
  197.0 4.2 %convolution_convert_fusion = bf16[480,6144]{1,0:T(8,128)(2,1)} fusion(bf16[480,256]{1,0:T(8,128)(2,1)S(1)} %fusion.8, bf16[1,256,6144]{2,1,0:T(8,128)(2,1)S(1)} %copy-done), kind=kOutput, calls=%fused_computation.2 | convolution fusion | flops 1512898560 | bytes 9289728 | tf_op jit(solution)/shard_map/dot_general | solution.py:115
  202.1 63.3 %reduce-scatter.2.cloned.1.call-done = bf16[480,1536]{1,0:T(8,128)(2,1)} async-done(((bf16[480,6144]{1,0:T(8,128)(2,1)}), bf16[480,1536]{1,0:T(8,128)(2,1)}) %reduce-scatter.2.cloned.1.call-update) | async-done | bytes 1474576 | tf_op jit(solution)/shard_map/reduce_scatter | solution.py:116
  265.4 7.5 %gather_fusion.1 = bf16[768,1536]{1,0:T(8,128)(2,1)} fusion(bf16[480,1536]{1,0:T(8,128)(2,1)} %reduce-scatter.2.cloned.1.call-done, s32[1024]{0:T(1024)S(1)} %pad_clamp_fusion), kind=kCustom, calls=%fused_computation.1 | custom fusion | bytes 4721664 | tf_op jit(solution)/shard_map/jit(_take)/gather | solution.py:124
  272.8 4.8 %gather.12 = bf16[32,2,1,12,1536]{4,3,1,0,2:T(8,128)(2,1)} reshape(bf16[768,1536]{1,0:T(8,128)(2,1)} %gather_fusion.1) | data formatting | bytes 4718592 | tf_op jit(solution)/shard_map/jit(_take)/gather | solution.py:124
  277.6 2.2 select_select_fusion
  279.8 1.3 copy.61
  281.1 5.6 %all_to_all.20 = bf16[32,2,1,12,1536]{4,0,3,2,1:T(8,128)(2,1)S(1)} all-to-all(bf16[32,2,1,12,1536]{4,0,3,2,1:T(8,128)(2,1)S(1)} %copy.61), channel_id=1, replica_groups=mesh['expert_0'=4,'expert_1'=8,'expert_2'=2,'mp'=4] {'expert_2'}, dimensions={1} | all-to-all | bytes 4718592 | tf_op jit(solution)/shard_map/all_to_all | solution.py:39
  286.7 3.8 %copy.62 = bf16[32,2,1,12,1536]{4,1,3,2,0:T(2,128)(2,1)} copy(bf16[32,2,1,12,1536]{4,0,3,2,1:T(8,128)(2,1)S(1)} %all_to_all.20) | data formatting | bytes 4718592 | tf_op jit(solution)/shard_map/all_to_all | solution.py:39
  290.5 10.4 %all-to-all-start.3 = ((bf16[32,2,1,12,1536]{4,1,3,2,0:T(2,128)(2,1)}), bf16[32,2,1,12,1536]{4,1,3,2,0:T(2,128)(2,1)}, u32[]{:S(2)}, u32[]{:S(2)}) async-start(bf16[32,2,1,12,1536]{4,1,3,2,0:T(2,128)(2,1)} %copy.62), calls=%async_computation.4 | async-start | bytes 4718592 | tf_op jit(solution)/shard_map/all_to_all | solution.py:39
  301.4 55.5 %all-to-all-done.3 = bf16[32,2,1,12,1536]{4,1,3,2,0:T(2,128)(2,1)} async-done(((bf16[32,2,1,12,1536]{4,1,3,2,0:T(2,128)(2,1)}), bf16[32,2,1,12,1536]{4,1,3,2,0:T(2,128)(2,1)}, u32[]{:S(2)}, u32[]{:S(2)}) %all-to-all-start.3) | async-done | bytes 2359328 | tf_op jit(solution)/shard_map/all_to_all | solution.py:39
  356.9 8.2 %convert_reduce_fusion = f32[32,12,1536]{2,1,0:T(8,128)S(1)} fusion(bf16[32,2,1,12,1536]{4,1,3,2,0:T(2,128)(2,1)} %all-to-all-done.3), kind=kLoop, calls=%fused_computation.3 | loop fusion | flops 1769472 | bytes 4718592 | tf_op jit(solution)/shard_map/reduce_sum | solution.py:134
  366.3 2.0 reshape.344
  368.3 2.1 convolution_convert_fusion.2
  (60 shorter events, 10.3 us)
Async XLA Ops:
  6.5 190.5 %copy-start = (bf16[1,256,6144]{2,1,0:T(8,128)(2,1)S(1)}, bf16[1,256,6144]{2,1,0:T(8,128)(2,1)}, u32[]{:S(2)}) copy-start(bf16[1,256,6144]{2,1,0:T(8,128)(2,1)} %param.11) | copy-start | bytes 9437188
  8.3 19.7 %all-to-all-start = ((s32[64,1,8]{2,1,0:T(1,128)}), s32[64,1,8]{2,1,0:T(1,128)S(1)}, u32[]{:S(2)}, u32[]{:S(2)}) async-start(s32[64,1,8]{2,1,0:T(1,128)} %broadcast_in_dim.86), calls=%async_computation | async-start | bytes 65536 | tf_op jit(solution)/shard_map/all_to_all | solution.py:20
  32.6 78.3 %all-to-all-start.1 = ((bf16[64,12,1536]{2,1,0:T(8,128)(2,1)}), bf16[64,12,1536]{2,1,0:T(8,128)(2,1)}, u32[]{:S(2)}, u32[]{:S(2)}) async-start(bf16[64,12,1536]{2,1,0:T(8,128)(2,1)} %bitcast.37), calls=%async_computation.1 | async-start | bytes 6291456 | tf_op jit(solution)/shard_map/all_to_all | solution.py:92
  40.0 149.1 %all-gather.2.cloned.1.call-start = ((), (), s32[]{:S(2)}) async-start(), calls=%async_computation.5 | async-start | bytes 7372800 | tf_op jit(solution)/shard_map/all_gather | solution.py:111
  124.9 140.4 %reduce-scatter.2.cloned.1.call-start = ((), (), s32[]{:S(2)}) async-start(), calls=%async_computation.6 | async-start | bytes 7372800 | tf_op jit(solution)/shard_map/reduce_scatter | solution.py:116
  189.1 5.5 %copy-start.2 = (bf16[480,6144]{1,0:T(8,128)(2,1)S(1)}, bf16[480,6144]{1,0:T(8,128)(2,1)}, u32[]{:S(2)}) copy-start(bf16[480,6144]{1,0:T(8,128)(2,1)} %all-gather.2.cloned.1.call-done) | copy-start | bytes 17694724
  189.1 6.2 %copy-start.3 = (bf16[1,6144,256]{2,1,0:T(8,128)(2,1)S(1)}, bf16[1,6144,256]{2,1,0:T(8,128)(2,1)}, u32[]{:S(2)}) copy-start(bf16[1,6144,256]{2,1,0:T(8,128)(2,1)} %param.10) | copy-start | bytes 9437188
  290.5 10.4 %copy-start.1 = (f32[24,2]{0,1:T(2,128)S(1)}, f32[24,2]{0,1:T(2,128)}, u32[]{:S(2)}) copy-start(f32[24,2]{0,1:T(2,128)} %param.7) | copy-start | bytes 580
  290.5 66.4 %all-to-all-start.3 = ((bf16[32,2,1,12,1536]{4,1,3,2,0:T(2,128)(2,1)}), bf16[32,2,1,12,1536]{4,1,3,2,0:T(2,128)(2,1)}, u32[]{:S(2)}, u32[]{:S(2)}) async-start(bf16[32,2,1,12,1536]{4,1,3,2,0:T(2,128)(2,1)} %copy.62), calls=%async_computation.4 | async-start | bytes 4718592 | tf_op jit(solution)/shard_map/all_to_all | solution.py:39
Sparse Core Ops, SparseCore 0:
  125.0 63.9 all-gather.1
  201.4 63.9 reduce-scatter.1
where the time goes:
time: 378 us; the launch traced here: 377 us
  waiting for transfers between devices  258 us (68%)
  local copies, waits for them, and re-layouts  36.2 us (10%)
  starting transfers between devices  30.2 us (8%)
  other arithmetic  18.5 us (5%)
  matrix products  14.6 us (4%)
  between operations  13.7 us (4%)
  blocking collectives  5.63 us (1%)
    all_to_all x1, waiting for transfers between devices, local(): lax.all_to_all(pack_rows(pick_tokens, tokens, group_size), EXPERT, split_...  68.9 us
    all_gather x1, waiting for transfers between devices, local(): shard_piece = lax.all_gather(in_rows, 'mp', axis=1, tiled=True)  63.9 us
    reduce_scatter x1, waiting for transfers between devices, local(): lax.psum_scatter(part_sum.astype(jnp.bfloat16), 'mp', scatter_dimension=1...  63.3 us
    all_to_all x1, waiting for transfers between devices, exchange_in_order(): lax.all_to_all(pieces, axes[k], split_axis=k, concat_axis=k, tiled=True)  55.5 us
    gather x2, local copies, waits for them, and re-layouts, local(): jnp.take(reduced, back_idx, axis=0)  12.2 us
    all_to_all x1, starting transfers between devices, copy_for_each(): lax.all_to_all(jnp.broadcast_to(value[None], (size, *value.shape)), axis,...  12.2 us
    all_to_all x1, starting transfers between devices, exchange_in_order(): lax.all_to_all(pieces, axes[k], split_axis=k, concat_axis=k, tiled=True)  10.4 us
    reduce_sum x2, other arithmetic, local(): jnp.sum(returned.reshape(EXPERTS, group_size, most_rows, out_width).astyp...  9.32 us
  transfers between devices with their start and end apart: 5, of which 5 were waited for; matrix products, arithmetic and copies ran while one was open for 1% of the time, Pallas kernels for 0%

commit v1 on v0

--- a/solution.py
+++ b/solution.py
@@ -108,7 +108,22 @@
     in_rows = jnp.where(
         slot_valid[:, None], jnp.take(arrived_rows, fetch_idx, axis=0), jnp.zeros((), jnp.bfloat16)
     )
-    shard_piece = lax.all_gather(in_rows, "mp", axis=1, tiled=True)
+    ways, here, step = (lax.axis_size("mp"), lax.axis_index("mp"), in_rows.shape[1])
+    dims = [n * ways if d == 1 else n for d, n in enumerate(in_rows.shape)]
+    shard_piece = lax.dynamic_update_slice_in_dim(
+        jnp.zeros(dims, in_rows.dtype), in_rows, here * step, axis=1
+    )
+    going_up = going_down = in_rows
+    for far in range(1, ways // 2 + 1):
+        going_up = lax.ppermute(going_up, "mp", [(d, (d + 1) % ways) for d in range(ways)])
+        shard_piece = lax.dynamic_update_slice_in_dim(
+            shard_piece, going_up, (here - far) % ways * step, axis=1
+        )
+        if 2 * far < ways:
+            going_down = lax.ppermute(going_down, "mp", [(d, (d - 1) % ways) for d in range(ways)])
+            shard_piece = lax.dynamic_update_slice_in_dim(
+                shard_piece, going_down, (here + far) % ways * step, axis=1
+            )
     gate_act = jnp.dot(shard_piece, gate_rows, preferred_element_type=jnp.float32)
     up_act = jnp.dot(shard_piece, up_rows, preferred_element_type=jnp.float32)
     hidden = activate(gate_act, up_act)

time: 378 us -> 386 us (1.021)
  local copies, waits for them, and re-layouts: 36.2 us -> 48.1 us
  waiting for transfers between devices: 258 us -> 253 us
    all_gather x1 -> x0, waiting for transfers between devices: 63.9 us -> none  [local(): shard_piece = lax.all_gather(in_rows, 'mp', axis=1, tiled=True)]
    ppermute x0 -> x3, waiting for transfers between devices: none -> 62.2 us  [the longest x2 62.1 us: local(): lax.ppermute(going_up, 'mp', [(d, (d + 1) % ways) for d in range(ways)])]
    dynamic_update_slice x0 -> x3, local copies, waits for them, and re-layouts: none -> 8.06 us  [the longest x2 5.25 us: local(): lax.dynamic_update_slice_in_dim(shard_piece, going_up, (here - far) % way...]
  transfers between devices with their start and end apart: 5 -> 7, of which waited for: 5 -> 6; matrix products, arithmetic and copies ran while one was open for 1% -> 2% of each run, Pallas kernels for 0% -> 0%
where the time goes in v1:
time: 386 us; the launch traced here: 385 us
  waiting for transfers between devices  253 us (66%)
  local copies, waits for them, and re-layouts  48.1 us (12%)
  starting transfers between devices  33.7 us (9%)
  other arithmetic  17.3 us (4%)
  matrix products  13.7 us (4%)
  between operations  13.7 us (4%)
  blocking collectives  5.63 us (1%)
    all_to_all x1, waiting for transfers between devices, local(): lax.all_to_all(pack_rows(pick_tokens, tokens, group_size), EXPERT, split_...  68.9 us
    ppermute x2, waiting for transfers between devices, local(): lax.ppermute(going_up, 'mp', [(d, (d + 1) % ways) for d in range(ways)])  62.1 us
    reduce_scatter x1, waiting for transfers between devices, local(): lax.psum_scatter(part_sum.astype(jnp.bfloat16), 'mp', scatter_dimension=1...  59.5 us
    all_to_all x1, waiting for transfers between devices, exchange_in_order(): lax.all_to_all(pieces, axes[k], split_axis=k, concat_axis=k, tiled=True)  55.5 us
    gather x2, local copies, waits for them, and re-layouts, local(): jnp.take(reduced, back_idx, axis=0)  12.2 us
    all_to_all x1, starting transfers between devices, copy_for_each(): lax.all_to_all(jnp.broadcast_to(value[None], (size, *value.shape)), axis,...  12.2 us
    all_to_all x1, starting transfers between devices, exchange_in_order(): lax.all_to_all(pieces, axes[k], split_axis=k, concat_axis=k, tiled=True)  10.3 us
    reduce_sum x2, other arithmetic, local(): jnp.sum(returned.reshape(EXPERTS, group_size, most_rows, out_width).astyp...  9.32 us
  transfers between devices with their start and end apart: 7, of which 6 were waited for; matrix products, arithmetic and copies ran while one was open for 2% of the time, Pallas kernels for 0%

profile of v1, /device:TPU:6, one launch (start us, length us, event | category | flops | bytes accessed | tf_op | source)
XLA Modules:
  0.0 384.9 jit_solution(6624097068224139420)
XLA Ops:
  8.3 12.2 %all-to-all-start = ((s32[64,1,8]{2,1,0:T(1,128)}), s32[64,1,8]{2,1,0:T(1,128)S(1)}, u32[]{:S(2)}, u32[]{:S(2)}) async-start(s32[64,1,8]{2,1,0:T(1,128)} %broadcast_in_dim.89), calls=%async_computation | async-start | bytes 65536 | tf_op jit(solution)/shard_map/all_to_all | solution.py:20
  21.3 6.7 %all-to-all-done = s32[64,1,8]{2,1,0:T(1,128)S(1)} async-done(((s32[64,1,8]{2,1,0:T(1,128)}), s32[64,1,8]{2,1,0:T(1,128)S(1)}, u32[]{:S(2)}, u32[]{:S(2)}) %all-to-all-start) | async-done | bytes 2080 | tf_op jit(solution)/shard_map/all_to_all | solution.py:20
  32.6 7.5 %all-to-all-start.1 = ((bf16[64,12,1536]{2,1,0:T(8,128)(2,1)}), bf16[64,12,1536]{2,1,0:T(8,128)(2,1)}, u32[]{:S(2)}, u32[]{:S(2)}) async-start(bf16[64,12,1536]{2,1,0:T(8,128)(2,1)} %bitcast.32), calls=%async_computation.1 | async-start | bytes 6291456 | tf_op jit(solution)/shard_map/all_to_all | solution.py:92
  41.9 68.9 %all-to-all-done.1 = bf16[64,12,1536]{2,1,0:T(8,128)(2,1)} async-done(((bf16[64,12,1536]{2,1,0:T(8,128)(2,1)}), bf16[64,12,1536]{2,1,0:T(8,128)(2,1)}, u32[]{:S(2)}, u32[]{:S(2)}) %all-to-all-start.1) | async-done | bytes 2359328 | tf_op jit(solution)/shard_map/all_to_all | solution.py:92
  110.9 4.9 %reshape.343 = bf16[768,1536]{1,0:T(8,128)(2,1)} reshape(bf16[64,12,1536]{2,1,0:T(8,128)(2,1)} %all-to-all-done.1) | data formatting | bytes 4718592 | tf_op jit(solution)/shard_map/reshape | solution.py:95
  115.8 6.3 %gather_fusion = bf16[480,1536]{1,0:T(8,128)(2,1)} fusion(bf16[768,1536]{1,0:T(8,128)(2,1)} %reshape.343, s32[1024]{0:T(1024)S(1)} %pad_clamp_fusion.1), kind=kCustom, calls=%fused_computation | custom fusion | bytes 2951040 | tf_op jit(solution)/shard_map/jit(_take)/gather | solution.py:109
  125.1 2.5 copy-done.2
  130.8 31.8 %collective-permute-done = bf16[480,1536]{1,0:T(8,128)(2,1)} collective-permute-done((bf16[480,1536]{1,0:T(8,128)(2,1)}, bf16[480,1536]{1,0:T(8,128)(2,1)}, u32[]{:S(2)}, u32[]{:S(2)}) %collective-permute-start) | collective-permute-done | bytes 1474592 | tf_op jit(solution)/shard_map/ppermute | solution.py:118
  163.1 2.6 constant_dynamic-update-slice_fusion.2
  165.7 2.8 constant_dynamic-update-slice_fusion.1
  168.5 30.3 %collective-permute-done.2 = bf16[480,1536]{1,0:T(8,128)(2,1)} collective-permute-done((bf16[480,1536]{1,0:T(8,128)(2,1)}, bf16[480,1536]{1,0:T(8,128)(2,1)}, u32[]{:S(2)}, u32[]{:S(2)}) %collective-permute-start.2) | collective-permute-done | bytes 1474592 | tf_op jit(solution)/shard_map/ppermute | solution.py:118
  198.9 2.6 constant_dynamic-update-slice_fusion
  201.5 4.6 %fusion.1 = f32[480,256]{1,0:T(8,128)S(1)} fusion(bf16[480,6144]{1,0:T(8,128)(2,1)} %constant_dynamic-update-slice_fusion, bf16[1,6144,256]{2,1,0:T(8,128)(2,1)S(1)} %copy-done.5), kind=kOutput, calls=%fused_computation.6 | convolution fusion | flops 1509949440 | bytes 9535488 | tf_op jit(solution)/shard_map/dot_general | solution.py:128
  208.5 4.3 %convolution_convert_fusion = bf16[480,6144]{1,0:T(8,128)(2,1)} fusion(bf16[1,256,6144]{2,1,0:T(8,128)(2,1)S(1)} %copy-done, f32[480,256]{1,0:T(8,128)S(1)} %fusion.1, f32[480,256]{1,0:T(8,128)S(1)} %fusion.3), kind=kOutput, calls=%fused_computation.2 | convolution fusion | flops 1513635840 | bytes 10027008 | tf_op jit(solution)/shard_map/dot_general | solution.py:130
  213.6 59.5 %reduce-scatter.2.cloned.1.call-done = bf16[480,1536]{1,0:T(8,128)(2,1)} async-done(((bf16[480,6144]{1,0:T(8,128)(2,1)}), bf16[480,1536]{1,0:T(8,128)(2,1)}) %reduce-scatter.2.cloned.1.call-update) | async-done | bytes 1474576 | tf_op jit(solution)/shard_map/reduce_scatter | solution.py:131
  273.1 7.5 %gather_fusion.1 = bf16[768,1536]{1,0:T(8,128)(2,1)} fusion(bf16[480,1536]{1,0:T(8,128)(2,1)} %reduce-scatter.2.cloned.1.call-done, s32[1024]{0:T(1024)S(1)} %pad_clamp_fusion), kind=kCustom, calls=%fused_computation.1 | custom fusion | bytes 4721664 | tf_op jit(solution)/shard_map/jit(_take)/gather | solution.py:139
  280.5 4.8 %gather.12 = bf16[32,2,1,12,1536]{4,3,1,0,2:T(8,128)(2,1)} reshape(bf16[768,1536]{1,0:T(8,128)(2,1)} %gather_fusion.1) | data formatting | bytes 4718592 | tf_op jit(solution)/shard_map/jit(_take)/gather | solution.py:139
  285.3 2.2 select_select_fusion
  288.8 5.6 %all_to_all.20 = bf16[32,2,1,12,1536]{4,0,3,2,1:T(8,128)(2,1)S(1)} all-to-all(bf16[32,2,1,12,1536]{4,0,3,2,1:T(8,128)(2,1)S(1)} %copy.61), channel_id=1, replica_groups=mesh['expert_0'=4,'expert_1'=8,'expert_2'=2,'mp'=4] {'expert_2'}, dimensions={1} | all-to-all | bytes 4718592 | tf_op jit(solution)/shard_map/all_to_all | solution.py:39
  294.4 3.8 copy.62
  298.2 10.3 %all-to-all-start.3 = ((bf16[32,2,1,12,1536]{4,1,3,2,0:T(2,128)(2,1)}), bf16[32,2,1,12,1536]{4,1,3,2,0:T(2,128)(2,1)}, u32[]{:S(2)}, u32[]{:S(2)}) async-start(bf16[32,2,1,12,1536]{4,1,3,2,0:T(2,128)(2,1)} %copy.62), calls=%async_computation.4 | async-start | bytes 4718592 | tf_op jit(solution)/shard_map/all_to_all | solution.py:39
  309.1 55.5 %all-to-all-done.3 = bf16[32,2,1,12,1536]{4,1,3,2,0:T(2,128)(2,1)} async-done(((bf16[32,2,1,12,1536]{4,1,3,2,0:T(2,128)(2,1)}), bf16[32,2,1,12,1536]{4,1,3,2,0:T(2,128)(2,1)}, u32[]{:S(2)}, u32[]{:S(2)}) %all-to-all-start.3) | async-done | bytes 2359328 | tf_op jit(solution)/shard_map/all_to_all | solution.py:39
  364.6 8.2 %convert_reduce_fusion = f32[32,12,1536]{2,1,0:T(8,128)S(1)} fusion(bf16[32,2,1,12,1536]{4,1,3,2,0:T(2,128)(2,1)} %all-to-all-done.3), kind=kLoop, calls=%fused_computation.3 | loop fusion | flops 1769472 | bytes 4718592 | tf_op jit(solution)/shard_map/reduce_sum | solution.py:149
  376.0 2.1 convolution_convert_fusion.2
  (73 shorter events, 23.8 us)
Async XLA Ops:
  6.5 202.0 %copy-start = (bf16[1,256,6144]{2,1,0:T(8,128)(2,1)S(1)}, bf16[1,256,6144]{2,1,0:T(8,128)(2,1)}, u32[]{:S(2)}) copy-start(bf16[1,256,6144]{2,1,0:T(8,128)(2,1)} %param.11) | copy-start | bytes 9437188
  8.3 19.7 %all-to-all-start = ((s32[64,1,8]{2,1,0:T(1,128)}), s32[64,1,8]{2,1,0:T(1,128)S(1)}, u32[]{:S(2)}, u32[]{:S(2)}) async-start(s32[64,1,8]{2,1,0:T(1,128)} %broadcast_in_dim.89), calls=%async_computation | async-start | bytes 65536 | tf_op jit(solution)/shard_map/all_to_all | solution.py:20
  32.6 78.3 %all-to-all-start.1 = ((bf16[64,12,1536]{2,1,0:T(8,128)(2,1)}), bf16[64,12,1536]{2,1,0:T(8,128)(2,1)}, u32[]{:S(2)}, u32[]{:S(2)}) async-start(bf16[64,12,1536]{2,1,0:T(8,128)(2,1)} %bitcast.32), calls=%async_computation.1 | async-start | bytes 6291456 | tf_op jit(solution)/shard_map/all_to_all | solution.py:92
  40.0 233.0 %reduce-scatter.2.cloned.1.call-start = ((), (), s32[]{:S(2)}) async-start(), calls=%async_computation.5 | async-start | bytes 7372800 | tf_op jit(solution)/shard_map/reduce_scatter | solution.py:131
  122.1 1.4 copy-start.1
  125.1 2.5 copy-start.2
  127.6 35.0 %collective-permute-start = (bf16[480,1536]{1,0:T(8,128)(2,1)}, bf16[480,1536]{1,0:T(8,128)(2,1)}, u32[]{:S(2)}, u32[]{:S(2)}) collective-permute-start(bf16[480,1536]{1,0:T(8,128)(2,1)} %get-tuple-element.11), channel_id=1, source_target_pairs={{0,1},{1,2},{2,3},{3,0},{4,5},{5,6},{6,7},{7,4},{8,9},{9,10},{10,1... | collective-permute-start | bytes 4423688 | tf_op jit(solution)/shard_map/ppermute | solution.py:118
  129.2 36.5 %collective-permute-start.1 = (bf16[480,1536]{1,0:T(8,128)(2,1)}, bf16[480,1536]{1,0:T(8,128)(2,1)}, u32[]{:S(2)}, u32[]{:S(2)}) collective-permute-start(bf16[480,1536]{1,0:T(8,128)(2,1)} %get-tuple-element.11), channel_id=1, source_target_pairs={{0,3},{1,0},{2,1},{3,2},{4,7},{5,4},{6,5},{7,6},{8,11},{9,8},{10,9... | collective-permute-start | bytes 4423688 | tf_op jit(solution)/shard_map/ppermute | solution.py:123
  162.7 36.2 %collective-permute-start.2 = (bf16[480,1536]{1,0:T(8,128)(2,1)}, bf16[480,1536]{1,0:T(8,128)(2,1)}, u32[]{:S(2)}, u32[]{:S(2)}) collective-permute-start(bf16[480,1536]{1,0:T(8,128)(2,1)} %collective-permute-done), channel_id=1, source_target_pairs={{0,1},{1,2},{2,3},{3,0},{4,5},{5,6},{6,7},{7,4},{8,9},{9,10},{10,1... | collective-permute-start | bytes 4423688 | tf_op jit(solution)/shard_map/ppermute | solution.py:118
  165.7 35.8 %copy-start.5 = (bf16[1,6144,256]{2,1,0:T(8,128)(2,1)S(1)}, bf16[1,6144,256]{2,1,0:T(8,128)(2,1)}, u32[]{:S(2)}) copy-start(bf16[1,6144,256]{2,1,0:T(8,128)(2,1)} %param.10) | copy-start | bytes 9437188
  201.5 4.6 %copy-start.3 = (bf16[480,6144]{1,0:T(8,128)(2,1)S(1)}, bf16[480,6144]{1,0:T(8,128)(2,1)}, u32[]{:S(2)}) copy-start(bf16[480,6144]{1,0:T(8,128)(2,1)} %constant_dynamic-update-slice_fusion) | copy-start | bytes 17694724
  201.5 5.3 %copy-start.6 = (bf16[1,6144,256]{2,1,0:T(8,128)(2,1)S(1)}, bf16[1,6144,256]{2,1,0:T(8,128)(2,1)}, u32[]{:S(2)}) copy-start(bf16[1,6144,256]{2,1,0:T(8,128)(2,1)} %param.9) | copy-start | bytes 9437188
  298.2 10.4 %copy-start.4 = (f32[24,2]{0,1:T(2,128)S(1)}, f32[24,2]{0,1:T(2,128)}, u32[]{:S(2)}) copy-start(f32[24,2]{0,1:T(2,128)} %param.7) | copy-start | bytes 580
  298.2 66.4 %all-to-all-start.3 = ((bf16[32,2,1,12,1536]{4,1,3,2,0:T(2,128)(2,1)}), bf16[32,2,1,12,1536]{4,1,3,2,0:T(2,128)(2,1)}, u32[]{:S(2)}, u32[]{:S(2)}) async-start(bf16[32,2,1,12,1536]{4,1,3,2,0:T(2,128)(2,1)} %copy.62), calls=%async_computation.4 | async-start | bytes 4718592 | tf_op jit(solution)/shard_map/all_to_all | solution.py:39
Sparse Core Ops, SparseCore 0:
  212.9 60.1 reduce-scatter.1
